TPU v7x, 32 devices: a 4x2x2 block of a 4x4x8 slice. The times are simulated.
32 devices in a mesh: dp: 4 (over y, z), tp: 8 (over x, core).
Axes of the slice: x: 4, y: 2, z: 2, core: 2. Of those that a mesh axis runs over, the one named last changes fastest.
The devices are a block of a 4x4x8 slice.
Arguments:
- query: bfloat16 [128, 64, 128], P('dp', 'tp'), parts along dimension 0
- k_cache: bfloat16 [128, 1024, 8, 128], P('dp', None, 'tp'), parts along dimension 0
- v_cache: bfloat16 [128, 1024, 8, 128], P('dp', None, 'tp'), parts along dimension 0
- k_new: bfloat16 [128, 8, 128], P('dp', 'tp'), parts along dimension 0
- v_new: bfloat16 [128, 8, 128], P('dp', 'tp'), parts along dimension 0
- lens: int32 [128], P('dp'), parts along dimension 0
Outputs:
- output 1: bfloat16 [128, 64, 128], P('dp', 'tp'), parts along dimension 0
- output 2: bfloat16 [128, 1024, 8, 128], P('dp', 'tp'), parts along dimension 0
- output 3: bfloat16 [128, 1024, 8, 128], P('dp', 'tp'), parts along dimension 0
There are 4 independent parts. A program takes and returns all parts, laid end to end along the dimension named above; each array names one.
All inputs are finite; a program needn't handle non-finite values.
Results may differ from a plain program's by a relative error of at most 0.00769032.
Values are sent between devices in bfloat16 or wider.
A program may use at most 768 MiB of HBM per device.

v0:
```python
import jax
import jax.numpy as jnp
from jax import lax
from jax.sharding import PartitionSpec as P

MASK_VALUE = -1e30


def solution(mesh):
    def local_step(query, k_cache, v_cache, k_new, v_new, lens):
        batch, seq_len, head_dim = k_cache.shape[0], k_cache.shape[1], k_cache.shape[3]
        positions = lax.broadcasted_iota(jnp.int32, (1, seq_len, 1, 1), 1)
        new_slot = positions == lens[:, None, None, None]
        k_upd = jnp.where(new_slot, k_new[:, None], k_cache)
        v_upd = jnp.where(new_slot, v_new[:, None], v_cache)
        k_seq = lax.all_to_all(k_upd, "tp", 1, 2, tiled=True)
        v_seq = lax.all_to_all(v_upd, "tp", 1, 2, tiled=True)
        q_all = lax.all_gather(query, "tp", axis=1, tiled=True)
        seq_local, kv_heads = k_seq.shape[1], k_seq.shape[2]
        q_heads = q_all.shape[1]
        q_grp = q_all.reshape(batch, kv_heads, q_heads // kv_heads, head_dim)
        scores = jnp.einsum("bhgd,bthd->bhgt", q_grp, k_seq, preferred_element_type=jnp.float32) * (head_dim ** -0.5)
        tok_pos = lax.axis_index("tp") * seq_local + lax.broadcasted_iota(jnp.int32, (1, 1, 1, seq_local), 3)
        valid = tok_pos <= lens[:, None, None, None]
        scores = jnp.where(valid, scores, MASK_VALUE)
        part_max = jnp.max(scores, axis=-1)
        weights = jnp.where(valid, jnp.exp(scores - part_max[..., None]), 0.0)
        part_sum = jnp.sum(weights, axis=-1)
        part_out = jnp.einsum("bhgt,bthd->bhgd", weights.astype(jnp.bfloat16), v_seq, preferred_element_type=jnp.float32)
        glob_max = lax.pmax(part_max, "tp")
        factor = jnp.exp(part_max - glob_max)
        stacked = jnp.concatenate([part_out * factor[..., None], (part_sum * factor)[..., None]], axis=-1)
        stacked = stacked.reshape(batch, q_heads, head_dim + 1)
        own_heads = lax.psum_scatter(stacked, "tp", scatter_dimension=1, tiled=True)
        attn_out = (own_heads[..., :head_dim] / own_heads[..., head_dim:]).astype(jnp.bfloat16)
        return attn_out, k_seq, v_seq

    head_spec = P("dp", "tp")
    entry_spec = P("dp", None, "tp")
    return jax.shard_map(local_step, mesh=mesh, in_specs=(head_spec, entry_spec, entry_spec, head_spec, head_spec, P("dp")), out_specs=(head_spec, P("dp", "tp"), P("dp", "tp")), check_vma=False)
```

profile of v0, /device:TPU:81, one launch (start us, length us, event | category | flops | bytes accessed | tf_op | source)
XLA Modules:
  0.0 361.2 jit_solution(2854646478955013414)
XLA Ops:
  7.2 0.7 iota_compare_fusion
  7.9 35.1 %copy_select_fusion = (bf16[32,1024,1,128]{3,0,2,1:T(8,128)(2,1)}, bf16[32,1024,1,128]{3,0,2,1:T(8,128)(2,1)S(1)}) fusion(bf16[32,1024,1,128]{3,1,2,0:T(8,128)(2,1)} %param.8, pred[32,1024]{0,1:T(8,128)(4,1)S(1)} %iota_compare_fusion, bf16[32,128]{1,0:T(8,128)(2,1)} %bitcast.32, bf16[32,1024,1,128]{3,1,2,0:T(8,128)(2,1)} %param.7, bf16[32,128]{1,0:T(8,128)(2,1)} %bitcast.33), kind=kLoop, calls=%fused_computation | loop fusion | flops 8388608 | bytes 33603584 | tf_op jit(solution)/shard_map/jit(_where)/select_n | solution.py:15
  43.1 99.4 %all_to_all.36 = bf16[32,1024,1,128]{3,0,2,1:T(8,128)(2,1)} all-to-all(bf16[32,1024,1,128]{3,0,2,1:T(8,128)(2,1)S(1)} %get-tuple-element.21), channel_id=1, replica_groups=mesh['dp'=4,'tp'=8] {'tp'}, dimensions={1} | all-to-all | bytes 16777216 | tf_op jit(solution)/shard_map/all_to_all | solution.py:16
  142.5 6.1 %all-to-all-start.1 = ((bf16[32,1024,1,128]{3,0,2,1:T(8,128)(2,1)}), bf16[32,1024,1,128]{3,0,2,1:T(8,128)(2,1)}, u32[]{:S(2)}, u32[]{:S(2)}) async-start(bf16[32,1024,1,128]{3,0,2,1:T(8,128)(2,1)} %get-tuple-element.20), calls=%async_computation.1 | async-start | bytes 16777216 | tf_op jit(solution)/shard_map/all_to_all | solution.py:17
  148.6 0.0 reduce-scatter.2.cloned.1.call-start
  148.6 0.1 broadcast_compare_fusion
  148.7 102.5 %all_gather.3 = bf16[32,64,128]{2,1,0:T(8,128)(2,1)S(1)} all-gather(bf16[32,8,128]{2,1,0:T(8,128)(2,1)S(1)} %copy-done), channel_id=1, replica_groups=mesh['dp'=4,'tp'=8] {'tp'}, dimensions={1}, use_global_device_ids=true | all-gather | bytes 589824 | tf_op jit(solution)/shard_map/all_gather | solution.py:18
  251.2 10.0 %copy.38 = bf16[32,1024,1,128]{3,1,0,2:T(8,128)(2,1)} copy(bf16[32,1024,1,128]{3,0,2,1:T(8,128)(2,1)} %all_to_all.36) | data formatting | bytes 16777216 | tf_op jit(solution)/shard_map/all_to_all | solution.py:16
  261.2 6.9 %fusion.13 = (f32[32,8,8]{2,1,0:T(8,128)S(1)}, f32[32,8,8,128]{3,2,1,0:T(8,128)S(1)}) fusion(bf16[32,128,8,128]{3,1,2,0:T(8,128)(2,1)} %bitcast.30, bf16[32,64,128]{2,1,0:T(8,128)(2,1)S(1)} %all_gather.3, pred[32,128]{1,0:T(8,128)(4,1)S(1)} %broadcast_compare_fusion), kind=kOutput, calls=%fused_computation.24 | convolution fusion | flops 67893248 | bytes 9973760 | tf_op jit(solution)/shard_map/bhgd,bthd->bhgt/dot_general | solution.py:22
  268.1 22.8 %pmax.7 = f32[32,8,8]{2,1,0:T(8,128)S(1)} all-reduce(f32[32,8,8]{2,1,0:T(8,128)S(1)} %get-tuple-element.22), channel_id=1, replica_groups=mesh['dp'=4,'tp'=8] {'tp'}, use_global_device_ids=true, to_apply=%region_1.2 | all-reduce | flops 2048 | bytes 16384 | tf_op jit(solution)/shard_map/pmax | solution.py:30
  290.8 0.7 fusion.3
  291.5 0.1 copy.41
  291.6 0.0 all-to-all-done.1
  291.6 10.0 %copy.40 = bf16[32,1024,1,128]{3,1,0,2:T(8,128)(2,1)} copy(bf16[32,1024,1,128]{3,0,2,1:T(8,128)(2,1)} %all-to-all-done.1) | data formatting | bytes 16777216 | tf_op jit(solution)/shard_map/all_to_all | solution.py:17
  301.7 4.7 %fusion = f32[32,64,128]{2,1,0:T(8,128)S(1)} fusion(bf16[32,128,8,128]{3,1,2,0:T(8,128)(2,1)} %bitcast.29, f32[32,8,8,128]{3,2,1,0:T(8,128)S(1)} %get-tuple-element.23, f32[32,8,8]{2,1,0:T(8,128)S(1)} %get-tuple-element.19, f32[32,8,8]{2,1,0:T(8,128)S(1)} %get-tuple-element.22, pred[32,128]{1,0:T(8,128)(4,1)S(1)} %broadcast_compare_fusion), kind=kOutput, calls=%fused_computation.4 | convolution fusion | flops 68157440 | bytes 10506240 | tf_op jit(solution)/shard_map/bhgt,bthd->bhgd/dot_general | solution.py:29
  306.4 4.4 %copy.42 = f32[32,64,128]{0,1,2:T(8,128)} copy(f32[32,64,128]{2,1,0:T(8,128)S(1)} %fusion) | data formatting | bytes 2097152 | tf_op jit(solution)/shard_map/concatenate | solution.py:32
  310.8 5.0 %pad_maximum_fusion = f32[32,64,129]{0,1,2:T(8,128)} fusion(f32[32,64,1]{0,1,2:T(8,128)S(1)} %bitcast.31, f32[32,64,128]{0,1,2:T(8,128)} %copy.42), kind=kLoop, calls=%fused_computation.2 | loop fusion | flops 264192 | bytes 2113536 | tf_op jit(solution)/shard_map/concatenate | solution.py:32
  315.8 0.1 reduce-scatter.2.cloned.1.call-update
  315.8 12.2 %copy.44 = bf16[32,128,8,128]{3,2,1,0:T(8,128)(2,1)} copy(bf16[32,128,8,128]{3,0,1,2:T(8,128)(2,1)} %bitcast.28) | data formatting | bytes 16777216
  328.0 12.2 %copy.45 = bf16[32,128,8,128]{3,2,1,0:T(8,128)(2,1)} copy(bf16[32,128,8,128]{3,0,1,2:T(8,128)(2,1)} %bitcast.18) | data formatting | bytes 16777216
  340.2 11.5 %reduce-scatter.2.cloned.1.call-done = f32[32,8,129]{0,1,2:T(8,128)} async-done(((f32[32,64,129]{0,1,2:T(8,128)}), f32[32,8,129]{0,1,2:T(8,128)}) %reduce-scatter.2.cloned.1.call-update) | async-done | bytes 132112 | tf_op jit(solution)/shard_map/reduce_scatter | solution.py:34
  351.7 0.7 slice_bitcast_fusion
  352.4 1.1 fusion.6
  353.5 0.8 copy.43
  (6 shorter events, 0.0 us)
Async XLA Ops:
  142.5 6.1 %copy-start.1 = (s32[32]{0:T(128)S(1)}, s32[32]{0:T(128)}, u32[]{:S(2)}) copy-start(s32[32]{0:T(128)} %param.11) | copy-start | bytes 388
  142.5 6.2 %copy-start = (bf16[32,8,128]{2,1,0:T(8,128)(2,1)S(1)}, bf16[32,8,128]{2,1,0:T(8,128)(2,1)}, u32[]{:S(2)}) copy-start(bf16[32,8,128]{2,1,0:T(8,128)(2,1)} %param.6) | copy-start | bytes 196612
  142.5 149.1 %all-to-all-start.1 = ((bf16[32,1024,1,128]{3,0,2,1:T(8,128)(2,1)}), bf16[32,1024,1,128]{3,0,2,1:T(8,128)(2,1)}, u32[]{:S(2)}, u32[]{:S(2)}) async-start(bf16[32,1024,1,128]{3,0,2,1:T(8,128)(2,1)} %get-tuple-element.20), calls=%async_computation.1 | async-start | bytes 16777216 | tf_op jit(solution)/shard_map/all_to_all | solution.py:17
  148.6 203.1 %reduce-scatter.2.cloned.1.call-start = ((), (), s32[]{:S(2)}) async-start(), calls=%async_computation.3 | async-start | bytes 4755456 | tf_op jit(solution)/shard_map/reduce_scatter | solution.py:34
Sparse Core Ops, SparseCore 0:
  315.9 35.7 reduce-scatter.1
where the time goes:
time: 363 us; the launch traced here: 361 us
  blocking collectives  225 us (62%)
  local copies, waits for them, and re-layouts  50.4 us (14%)
  other arithmetic  42.7 us (12%)
  between operations  14.1 us (4%)
  matrix products  11.6 us (3%)
  waiting for transfers between devices  11.6 us (3%)
  starting transfers between devices  6.09 us (2%)
    all_gather x1, blocking collectives, local_step(): q_all = lax.all_gather(query, 'tp', axis=1, tiled=True)  102 us
    all_to_all x1, blocking collectives, local_step(): k_seq = lax.all_to_all(k_upd, 'tp', 1, 2, tiled=True)  99.4 us
    select_n x1, other arithmetic, local_step(): v_upd = jnp.where(new_slot, v_new[:, None], v_cache)  35.1 us
    unnamed x7, local copies, waits for them, and re-layouts  25.2 us
    pmax x1, blocking collectives, local_step(): glob_max = lax.pmax(part_max, 'tp')  22.8 us
    reduce_scatter x1, waiting for transfers between devices, local_step(): own_heads = lax.psum_scatter(stacked, 'tp', scatter_dimension=1, tiled=True)  11.5 us
    all_to_all x1, local copies, waits for them, and re-layouts, local_step(): v_seq = lax.all_to_all(v_upd, 'tp', 1, 2, tiled=True)  10 us
    all_to_all x1, local copies, waits for them, and re-layouts, local_step(): k_seq = lax.all_to_all(k_upd, 'tp', 1, 2, tiled=True)  10 us
  transfers between devices with their start and end apart: 2, of which 1 were waited for; matrix products, arithmetic and copies ran while one was open for 12% of the time, Pallas kernels for 0%

commit v1 on v0

v1 whole, which is shorter than its diff:
```python
import functools
import jax
import jax.numpy as jnp
from jax import lax
from jax.experimental import pallas as pl
from jax.experimental.pallas import tpu as pltpu
from jax.sharding import PartitionSpec as P

MASK_VALUE = -1e30
MESH = pl.DeviceIdType.MESH
REQS = 2


def exchange_kernel(n, lens_ref, q_ref, kn_ref, vn_ref, k_hbm, v_hbm,
                    out_ref, k_out, v_out,
                    recv, new_recv, new_all, new_own, k_buf, v_buf,
                    send_sem, recv_sem, new_send_sem, new_recv_sem, kv_sem):
    batch, seq_len, head_dim = k_hbm.shape
    seq_local = seq_len // n
    chunks = batch // REQS
    me = lax.axis_index("tp")
    group = lax.axis_index("dp")
    caches = (k_hbm, v_hbm)
    outs = (k_out, v_out)

    def peer(j):
        return lax.rem(me + j, n)

    barrier = pltpu.get_barrier_semaphore()
    for j in range(1, n):
        pl.semaphore_signal(barrier, inc=1, device_id=(group, peer(j)), device_id_type=MESH)
    pl.semaphore_wait(barrier, n - 1)

    def unit_copy(c, kv, j):
        dst_dev = peer(j)
        src = caches[kv].at[pl.ds(c * REQS, REQS), pl.ds(pl.multiple_of(dst_dev * seq_local, seq_local), seq_local)]
        dst = recv.at[c, kv, me]
        if j == 0:
            return pltpu.make_async_copy(src, dst, recv_sem.at[c, kv])
        return pltpu.make_async_remote_copy(src, dst, send_sem.at[c, kv], recv_sem.at[c, kv],
                                            device_id=(group, dst_dev), device_id_type=MESH)

    def new_copy(kv, j):
        src = (kn_ref, vn_ref)[kv]
        return pltpu.make_async_remote_copy(src, new_recv.at[kv, me], new_send_sem, new_recv_sem,
                                            device_id=(group, peer(j)), device_id_type=MESH)

    for kv in range(2):
        for j in range(1, n):
            new_copy(kv, j).start()

    def start_unit(c, carry):
        for kv in range(2):
            for j in (4, 3, 5, 2, 6, 1, 7, 0):
                unit_copy(c, kv, j).start()
        return carry

    lax.fori_loop(0, chunks, start_unit, 0)

    for kv in range(2):
        new_own[kv] = (kn_ref, vn_ref)[kv][...].astype(jnp.float32)

    def load(b, slot):
        return (pltpu.make_async_copy(k_hbm.at[b], k_buf.at[slot], kv_sem.at[slot, 0]),
                pltpu.make_async_copy(v_hbm.at[b], v_buf.at[slot], kv_sem.at[slot, 1]))

    for cp in load(0, 0):
        cp.start()
    scale = head_dim ** -0.5
    pos = lax.broadcasted_iota(jnp.int32, (1, seq_len), 1)

    def attend(b, carry):
        slot = lax.rem(b, 2)

        @pl.when(b + 1 < batch)
        def _():
            for cp in load(b + 1, 1 - slot):
                cp.start()

        for cp in load(b, slot):
            cp.wait()
        length = lens_ref[b]
        q = q_ref[b]
        qf = q.astype(jnp.float32)
        s = lax.dot_general(q, k_buf[slot], (((1,), (1,)), ((), ())), preferred_element_type=jnp.float32) * scale
        s_new = jnp.sum(qf * new_own[0, pl.ds(b, 1), :], axis=1, keepdims=True) * scale
        s = jnp.where(pos < length, s, MASK_VALUE)
        m = jnp.maximum(jnp.max(s, axis=1, keepdims=True), s_new)
        e = jnp.where(pos < length, jnp.exp(s - m), 0.0)
        e_new = jnp.exp(s_new - m)
        denom = jnp.sum(e, axis=1, keepdims=True) + e_new
        p = (e / denom).astype(jnp.bfloat16)
        p_new = (e_new / denom).astype(jnp.bfloat16).astype(jnp.float32)
        o = lax.dot_general(p, v_buf[slot], (((1,), (0,)), ((), ())), preferred_element_type=jnp.float32)
        o = o + p_new * new_own[1, pl.ds(b, 1), :]
        out_ref[b] = o.astype(jnp.bfloat16)
        return carry

    lax.fori_loop(0, batch, attend, 0)

    moved = new_recv.at[:, pl.ds(0, n - 1)]
    pltpu.make_async_copy(moved, moved, new_send_sem).wait()
    pltpu.make_async_copy(moved, moved, new_recv_sem).wait()
    for kv in range(2):
        new_recv[kv, me] = (kn_ref, vn_ref)[kv][...]
        new_all[kv] = jnp.swapaxes(new_recv[kv].astype(jnp.float32), 0, 1)

    tok = lax.broadcasted_iota(jnp.int32, (seq_local, n, head_dim), 0)

    def finish(c, carry):
        for kv in range(2):
            pltpu.make_async_copy(recv.at[c, kv], recv.at[c, kv], recv_sem.at[c, kv]).wait()
            for r in range(REQS):
                b = c * REQS + r
                at = lens_ref[b] - me * seq_local
                x = jnp.swapaxes(recv[c, kv, :, r].astype(jnp.float32), 0, 1)
                x = jnp.where(tok == at, new_all[kv, b][None], x)
                outs[kv][b] = x.astype(jnp.bfloat16)
        return carry

    lax.fori_loop(0, chunks, finish, 0)

    def drain(c, carry):
        for kv in range(2):
            sent = recv.at[c, kv, pl.ds(0, n - 1)]
            pltpu.make_async_copy(sent, sent, send_sem.at[c, kv]).wait()
        return carry

    lax.fori_loop(0, chunks, drain, 0)


def solution(mesh):
    n = mesh.shape["tp"]

    def local_step(query, k_cache, v_cache, k_new, v_new, lens):
        batch, seq_len, kv_heads, head_dim = k_cache.shape
        group = query.shape[1]
        chunks = batch // REQS
        seq_local = seq_len // n
        vmem = pl.BlockSpec(memory_space=pltpu.VMEM)
        anym = pl.BlockSpec(memory_space=pl.ANY)
        cache_out = jax.ShapeDtypeStruct((batch, seq_local, n * kv_heads, head_dim), k_cache.dtype)
        return pl.pallas_call(
            functools.partial(exchange_kernel, n),
            out_shape=(jax.ShapeDtypeStruct(query.shape, query.dtype), cache_out, cache_out),
            in_specs=[pl.BlockSpec(memory_space=pltpu.SMEM), vmem, vmem, vmem, anym, anym],
            out_specs=(vmem, vmem, vmem),
            scratch_shapes=[
                pltpu.VMEM((chunks, 2, n, REQS, seq_local, head_dim), jnp.bfloat16),
                pltpu.VMEM((2, n, batch, head_dim), jnp.bfloat16),
                pltpu.VMEM((2, batch, n, head_dim), jnp.float32),
                pltpu.VMEM((2, batch, head_dim), jnp.float32),
                pltpu.VMEM((2, seq_len, head_dim), jnp.bfloat16),
                pltpu.VMEM((2, seq_len, head_dim), jnp.bfloat16),
                pltpu.SemaphoreType.DMA((chunks, 2)),
                pltpu.SemaphoreType.DMA((chunks, 2)),
                pltpu.SemaphoreType.DMA,
                pltpu.SemaphoreType.DMA,
                pltpu.SemaphoreType.DMA((2, 2)),
            ],
            compiler_params=pltpu.CompilerParams(
                collective_id=0, has_side_effects=True, vmem_limit_bytes=62 * 1024 * 1024
            ),
            name="exchange",
        )(lens, query, k_new.reshape(batch, head_dim), v_new.reshape(batch, head_dim),
          k_cache.reshape(batch, seq_len, head_dim), v_cache.reshape(batch, seq_len, head_dim))

    head_spec = P("dp", "tp")
    entry_spec = P("dp", None, "tp")
    return jax.shard_map(local_step, mesh=mesh, in_specs=(head_spec, entry_spec, entry_spec, head_spec, head_spec, P("dp")), out_specs=(head_spec, P("dp", "tp"), P("dp", "tp")), check_vma=False)
```

time: 363 us -> 213 us (0.59)
  blocking collectives: 225 us -> 0 us
  Pallas kernels: 0 us -> 195 us
  other arithmetic: 42.7 us -> 0 us
  local copies, waits for them, and re-layouts: 50.4 us -> 16.8 us
  between operations: 14.1 us -> 0.64 us
  matrix products: 11.6 us -> 0 us
  waiting for transfers between devices: 11.6 us -> 0 us
  starting transfers between devices: 6.09 us -> 0 us
    pallas_call x0 -> x1, Pallas kernels: none -> 195 us  [local_step(): pl.pallas_call(functools.partial(exchange_kernel, n), out_shape=(jax.Shap...]
    all_gather x1 -> x0, blocking collectives: 102 us -> none  [local_step(): q_all = lax.all_gather(query, 'tp', axis=1, tiled=True)]
    all_to_all x1 -> x0, blocking collectives: 99.4 us -> none  [local_step(): k_seq = lax.all_to_all(k_upd, 'tp', 1, 2, tiled=True)]
    select_n x1 -> x0, other arithmetic: 35.1 us -> none  [local_step(): v_upd = jnp.where(new_slot, v_new[:, None], v_cache)]
    pmax x1 -> x0, blocking collectives: 22.8 us -> none  [local_step(): glob_max = lax.pmax(part_max, 'tp')]
    all_to_all x2 -> x0, local copies, waits for them, and re-layouts: 20 us -> none  [the longest x1 10 us: local_step(): v_seq = lax.all_to_all(v_upd, 'tp', 1, 2, tiled=True)]
    dot_general x2 -> x0, matrix products: 11.6 us -> none  [the longest x1 6.89 us: local_step(): jnp.einsum('bhgd,bthd->bhgt', q_grp, k_seq, preferred_element_type=jnp.fl...]
    reduce_scatter x1 -> x0, waiting for transfers between devices: 11.5 us -> none  [local_step(): own_heads = lax.psum_scatter(stacked, 'tp', scatter_dimension=1, tiled=True)]
  transfers between devices with their start and end apart: 2 -> 0, of which waited for: 1 -> 0; matrix products, arithmetic and copies ran while one was open for 12% -> 0% of each run, Pallas kernels for 0% -> 0%
where the time goes in v1:
time: 213 us
  Pallas kernels  195 us (92%)
  local copies, waits for them, and re-layouts  16.8 us (8%)
    pallas_call x1, Pallas kernels, local_step(): pl.pallas_call(functools.partial(exchange_kernel, n), out_shape=(jax.Shap...  195 us
    unnamed x3, local copies, waits for them, and re-layouts  16.8 us

profile of v1, /device:TPU:81, one launch (start us, length us, event | category | flops | bytes accessed | tf_op | source)
XLA Modules:
  0.0 212.6 jit_solution(7694426936126013681)
XLA Ops:
  0.6 195.1 %exchange.1 = (bf16[32,8,128]{2,1,0:T(8,128)(2,1)}, bf16[32,128,8,128]{3,2,1,0:T(8,128)(2,1)}, bf16[32,128,8,128]{3,2,1,0:T(8,128)(2,1)}) custom-call(s32[32]{0:T(128)} %lens_ref.1, bf16[32,8,128]{2,1,0:T(8,128)(2,1)} %q_ref.1, bf16[32,128]{1,0:T(8,128)(2,1)} %bitcast.6, bf16[32,128]{1,0:T(8,128)(2,1)} %bitcast.7, bf16[32,1024,128]{2,1,0:T(8,128)(2,1)} %bitcast.4, ...), custom_call_target="tpu_custom_call" | custom-call | tf_op jit(solution)/shard_map/exchange/pallas_call | solution.py:143
  195.8 1.5 copy.12
  197.3 7.7 %copy.13 = bf16[32,128,8,128]{3,2,1,0:T(8,128)(2,1)} copy(bf16[32,128,8,128]{3,2,1,0:T(8,128)(2,1)} %get-tuple-element.7) | data formatting | bytes 16777216
  204.9 7.7 %copy.14 = bf16[32,128,8,128]{3,2,1,0:T(8,128)(2,1)} copy(bf16[32,128,8,128]{3,2,1,0:T(8,128)(2,1)} %get-tuple-element.8) | data formatting | bytes 16777216

commit v2 on v0

v2 whole, which is shorter than its diff:
```python
import functools
import jax
import jax.numpy as jnp
from jax import lax
from jax.experimental import pallas as pl
from jax.experimental.pallas import tpu as pltpu
from jax.sharding import PartitionSpec as P

MASK_VALUE = -1e30
MESH = pl.DeviceIdType.MESH
CHUNKS = (1, 1, 2, 4, 4, 4, 4, 4, 4, 2, 1, 1)
STORES = 4
LOADS = (1, 7, 8, 16)
ARRIVALS = (8, 8, 8, 4, 2, 1, 1)
HOPS = (4, 5, 3, 2, 6, 7, 1)


def spans(total, sizes):
    out, start = [], 0
    while start < total:
        size = min(sizes[min(len(out), len(sizes) - 1)], total - start)
        out.append(pl.ds(start, size))
        start += size
    return out


def span_of(total, sizes, b):
    return sum(b >= s.start for s in spans(total, sizes)[1:])


def exchange_kernel(n, lens_hbm, q_hbm, kn_hbm, vn_hbm, k_hbm, v_hbm,
                    out_ref, k_out, v_out,
                    lens_ref, q_ref, new_in, new_f32, kv, recv,
                    send_sem, recv_sem, load_sem, in_sem):
    batch, seq_len, head_dim = k_hbm.shape
    seq_local = seq_len // n
    me = lax.axis_index("tp")
    group = lax.axis_index("dp")
    outs = (k_out, v_out)

    barrier = pltpu.get_barrier_semaphore()
    for j in HOPS:
        pl.semaphore_signal(barrier, inc=1, device_id=(group, lax.rem(me + j, n)), device_id_type=MESH)

    def whole(ref, sem):
        return pltpu.make_async_copy(ref, ref, sem)

    small = (pltpu.make_async_copy(lens_hbm, lens_ref, in_sem.at[0]),
             pltpu.make_async_copy(kn_hbm, new_in.at[0], in_sem.at[1]),
             pltpu.make_async_copy(vn_hbm, new_in.at[1], in_sem.at[1]))
    query = pltpu.make_async_copy(q_hbm, q_ref, in_sem.at[2])
    load_spans = spans(batch, LOADS)

    def start_load(g):
        reqs = load_spans[g]
        pltpu.make_async_copy(k_hbm.at[reqs], kv.at[reqs, 0], load_sem.at[g]).start()
        pltpu.make_async_copy(v_hbm.at[reqs], kv.at[reqs, 1], load_sem.at[g]).start()

    for cp in small:
        cp.start()
    start_load(0)
    small[0].wait()
    whole(new_in, in_sem.at[1]).wait()
    new_f32[...] = new_in[...].astype(jnp.float32)

    row = lax.broadcasted_iota(jnp.int32, (seq_len, head_dim), 0)

    def insert_one(b, carry):
        at = lens_ref[b]
        for i in range(2):
            new = new_f32[i, pl.ds(b, 1), :].astype(kv.dtype)
            kv[b, i] = jnp.where(row == at, new, kv[b, i])
            recv[b, i, me] = kv[b, i, pl.ds(pl.multiple_of(me * seq_local, seq_local), seq_local)]
        return carry

    chunk_spans = spans(batch, CHUNKS)

    def insert(c):
        if c < len(chunk_spans):
            reqs = chunk_spans[c]
            for g, load in enumerate(load_spans):
                if load.start == reqs.start:
                    whole(kv.at[load], load_sem.at[g]).wait()
            lax.fori_loop(reqs.start, reqs.start + reqs.size, insert_one, 0)

    def send(c):
        reqs = chunk_spans[c]
        for j in HOPS:
            peer = lax.rem(me + j, n)
            pltpu.make_async_remote_copy(
                kv.at[reqs, :, pl.ds(pl.multiple_of(peer * seq_local, seq_local), seq_local)],
                recv.at[reqs, :, me], send_sem, recv_sem.at[span_of(batch, ARRIVALS, reqs.start)],
                device_id=(group, peer), device_id_type=MESH).start()

    insert(0)
    for g in range(1, len(load_spans)):
        start_load(g)
    query.start()
    pl.semaphore_wait(barrier, n - 1)
    send(0)
    insert(1)
    for c in range(1, len(chunk_spans)):
        insert(c + 1)
        send(c)
    query.wait()

    scale = head_dim ** -0.5
    pos = lax.broadcasted_iota(jnp.int32, (1, seq_len), 1)

    def attend(b, carry):
        s = lax.dot_general(q_ref[b], kv[b, 0], (((1,), (1,)), ((), ())), preferred_element_type=jnp.float32) * scale
        valid = pos <= lens_ref[b]
        s = jnp.where(valid, s, MASK_VALUE)
        e = jnp.exp(s - jnp.max(s, axis=1, keepdims=True))
        p = (e / jnp.sum(e, axis=1, keepdims=True)).astype(kv.dtype)
        o = lax.dot_general(p, kv[b, 1], (((1,), (0,)), ((), ())), preferred_element_type=jnp.float32)
        out_ref[b] = o.astype(out_ref.dtype)
        return carry

    lax.fori_loop(0, batch, attend, 0)

    def finish(b, carry):
        for i in range(2):
            x = jnp.swapaxes(recv[b, i].astype(jnp.float32), 0, 1)
            outs[i][b] = x.astype(kv.dtype)
        return carry

    for g, reqs in enumerate(spans(batch, ARRIVALS)):
        whole(recv.at[reqs, :, pl.ds(0, n - 1)], recv_sem.at[g]).wait()
        lax.fori_loop(reqs.start, reqs.start + reqs.size, finish, 0)

    whole(recv.at[:, :, pl.ds(0, n - 1)], send_sem).wait()


def store_kernel(out_in, k_in, v_in, out_hbm, k_hbm, v_hbm, sem):
    step = k_in.shape[0] // STORES
    pltpu.make_async_copy(out_in, out_hbm, sem.at[2]).start()
    for p in range(STORES):
        part = pl.ds(p * step, step)
        pltpu.make_async_copy(k_in.at[part], k_hbm.at[part], sem.at[0]).start()
        pltpu.make_async_copy(v_in.at[part], v_hbm.at[part], sem.at[1]).start()
    for i, ref in enumerate((k_in, v_in, out_in)):
        pltpu.make_async_copy(ref, ref, sem.at[i]).wait()


def solution(mesh):
    n = mesh.shape["tp"]

    def local_step(query, k_cache, v_cache, k_new, v_new, lens):
        batch, seq_len, kv_heads, head_dim = k_cache.shape
        seq_local = seq_len // n
        dtype = k_cache.dtype
        cache_out = pltpu.VMEM((batch, seq_local, n * kv_heads, head_dim), dtype)
        hbm = pl.BlockSpec(memory_space=pltpu.HBM)
        vmem = pl.BlockSpec(memory_space=pltpu.VMEM)
        held = pl.pallas_call(
            functools.partial(exchange_kernel, n),
            out_shape=(pltpu.VMEM(query.shape, query.dtype), cache_out, cache_out),
            in_specs=[hbm] * 6,
            out_specs=(vmem,) * 3,
            scratch_shapes=[
                pltpu.SMEM((batch,), jnp.int32),
                pltpu.VMEM(query.shape, query.dtype),
                pltpu.VMEM((2, batch, head_dim), dtype),
                pltpu.VMEM((2, batch, head_dim), jnp.float32),
                pltpu.VMEM((batch, 2, seq_len, head_dim), dtype),
                pltpu.VMEM((batch, 2, n, seq_local, head_dim), dtype),
                pltpu.SemaphoreType.DMA,
                pltpu.SemaphoreType.DMA((len(spans(batch, ARRIVALS)),)),
                pltpu.SemaphoreType.DMA((len(spans(batch, LOADS)),)),
                pltpu.SemaphoreType.DMA((3,)),
            ],
            compiler_params=pltpu.CompilerParams(
                collective_id=0, has_side_effects=True, vmem_limit_bytes=40 * 1024 * 1024
            ),
            name="exchange",
        )(lens, query, k_new.reshape(batch, head_dim), v_new.reshape(batch, head_dim),
          k_cache.reshape(batch, seq_len, head_dim), v_cache.reshape(batch, seq_len, head_dim))
        held = [pltpu.with_memory_space_constraint(h, pltpu.VMEM) for h in held]
        return pl.pallas_call(
            store_kernel,
            out_shape=tuple(jax.ShapeDtypeStruct(h.shape, h.dtype) for h in held),
            in_specs=[vmem] * 3,
            out_specs=(hbm,) * 3,
            scratch_shapes=[pltpu.SemaphoreType.DMA((3,))],
            compiler_params=pltpu.CompilerParams(vmem_limit_bytes=1024 * 1024),
            name="store",
        )(*held)

    head_spec = P("dp", "tp")
    entry_spec = P("dp", None, "tp")
    return jax.shard_map(local_step, mesh=mesh, in_specs=(head_spec, entry_spec, entry_spec, head_spec, head_spec, P("dp")), out_specs=(head_spec, P("dp", "tp"), P("dp", "tp")), check_vma=False)
```

time: 363 us -> 193 us (0.53)
  blocking collectives: 225 us -> 0 us
  Pallas kernels: 0 us -> 192 us
  local copies, waits for them, and re-layouts: 50.4 us -> 0 us
  other arithmetic: 42.7 us -> 0 us
  between operations: 14.1 us -> 0.64 us
  matrix products: 11.6 us -> 0 us
  waiting for transfers between devices: 11.6 us -> 0 us
  starting transfers between devices: 6.09 us -> 0 us
    pallas_call x0 -> x2, Pallas kernels: none -> 192 us  [the longest x1 186 us: local_step(): pl.pallas_call(functools.partial(exchange_kernel, n), out_shape=(pltpu.VM...]
    all_gather x1 -> x0, blocking collectives: 102 us -> none  [local_step(): q_all = lax.all_gather(query, 'tp', axis=1, tiled=True)]
    all_to_all x1 -> x0, blocking collectives: 99.4 us -> none  [local_step(): k_seq = lax.all_to_all(k_upd, 'tp', 1, 2, tiled=True)]
    select_n x1 -> x0, other arithmetic: 35.1 us -> none  [local_step(): v_upd = jnp.where(new_slot, v_new[:, None], v_cache)]
    unnamed x7 -> x0, local copies, waits for them, and re-layouts: 25.2 us -> none
    pmax x1 -> x0, blocking collectives: 22.8 us -> none  [local_step(): glob_max = lax.pmax(part_max, 'tp')]
    all_to_all x2 -> x0, local copies, waits for them, and re-layouts: 20 us -> none  [the longest x1 10 us: local_step(): v_seq = lax.all_to_all(v_upd, 'tp', 1, 2, tiled=True)]
    dot_general x2 -> x0, matrix products: 11.6 us -> none  [the longest x1 6.89 us: local_step(): jnp.einsum('bhgd,bthd->bhgt', q_grp, k_seq, preferred_element_type=jnp.fl...]
  transfers between devices with their start and end apart: 2 -> 0, of which waited for: 1 -> 0; matrix products, arithmetic and copies ran while one was open for 12% -> 0% of each run, Pallas kernels for 0% -> 0%
where the time goes in v2:
time: 193 us
  Pallas kernels  192 us (99%)
    pallas_call x1, Pallas kernels, local_step(): pl.pallas_call(functools.partial(exchange_kernel, n), out_shape=(pltpu.VM...  186 us
    pallas_call x1, Pallas kernels, local_step(): pl.pallas_call(store_kernel, out_shape=tuple((jax.ShapeDtypeStruct(h.shap...  5.9 us

profile of v2, /device:TPU:81, one launch (start us, length us, event | category | flops | bytes accessed | tf_op | source)
XLA Modules:
  0.0 192.9 jit_solution(3309259102971496997)
XLA Ops:
  0.6 186.3 %exchange.1 = (bf16[32,8,128]{2,1,0:T(8,128)(2,1)S(1)}, bf16[32,128,8,128]{3,2,1,0:T(8,128)(2,1)S(1)}, bf16[32,128,8,128]{3,2,1,0:T(8,128)(2,1)S(1)}) custom-call(s32[32]{0:T(128)} %lens_hbm.1, bf16[32,8,128]{2,1,0:T(8,128)(2,1)} %q_hbm.1, bf16[32,128]{1,0:T(8,128)(2,1)} %bitcast.6, bf16[32,128]{1,0:T(8,128)(2,1)} %bitcast.7, ...), custom_call_target="tpu_custom_call" | custom-call | tf_op jit(solution)/shard_map/exchange/pallas_call | solution.py:156
  187.0 5.9 %store.1 = (bf16[32,8,128]{2,1,0:T(8,128)(2,1)}, bf16[32,128,8,128]{3,2,1,0:T(8,128)(2,1)}, bf16[32,128,8,128]{3,2,1,0:T(8,128)(2,1)}) custom-call(bf16[32,8,128]{2,1,0:T(8,128)(2,1)S(1)} %get-tuple-element.6.out_in, bf16[32,128,8,128]{3,2,1,0:T(8,128)(2,1)S(1)} %get-tuple-element.7.k_in, bf16[32,128,8,128]{3,2,1,0:T(8,128)(2,1)S(1)} %get-tuple-element.8.v_in), custom_call_target="tpu_custom_call" | custom-call | tf_op jit(solution)/shard_map/store/pallas_call | solution.py:180

commit v3 on v0

v3 whole, which is shorter than its diff:
```python
import functools
import jax
import jax.numpy as jnp
from jax import lax
from jax.experimental import pallas as pl
from jax.experimental.pallas import tpu as pltpu
from jax.sharding import PartitionSpec as P

MASK_VALUE = -1e30
VMEM_BYTES = 67043328
LESS_BYTES = VMEM_BYTES - 1536 * 1024
TILE = 16
PIECES = (4, 4, 10, 10, 3, 1)
EARLY = 2
HOPS = (4, 5, 3, 6, 2, 7, 1)


def whole(ref, sem):
    return pltpu.make_async_copy(ref, ref, sem)


def pack_kernel(n, reqs, hops, after, lens_hbm, kn_hbm, vn_hbm, k_hbm, v_hbm, *refs):
    blocks = refs[after:after + len(hops)]
    lens_ref, new_in, new_f32, kv, in_sem, load_sem, out_sem = refs[after + len(hops):]
    seq_len, head_dim = k_hbm.shape[1:]
    seq_local = seq_len // n
    me = lax.axis_index("tp")
    small = (pltpu.make_async_copy(lens_hbm, lens_ref, in_sem.at[0]),
             pltpu.make_async_copy(kn_hbm, new_in.at[0], in_sem.at[1]),
             pltpu.make_async_copy(vn_hbm, new_in.at[1], in_sem.at[1]))
    for cp in small:
        cp.start()
    starts = [lax.rem(me + j, n) * seq_local for j in hops]
    for h, first in enumerate(starts):
        rows = pl.ds(pl.multiple_of(first, seq_local), seq_local)
        pltpu.make_async_copy(k_hbm.at[reqs, rows], kv.at[h, :, 0], load_sem.at[h]).start()
        pltpu.make_async_copy(v_hbm.at[reqs, rows], kv.at[h, :, 1], load_sem.at[h]).start()
    small[0].wait()
    whole(new_in, in_sem.at[1]).wait()
    new_f32[...] = new_in[...].astype(jnp.float32)
    row = lax.broadcasted_iota(jnp.int32, (TILE, head_dim), 0)
    for h, first in enumerate(starts):
        whole(kv.at[h], load_sem.at[h]).wait()

        def insert(r, carry):
            at = lens_ref[reqs.start + r] - first
            tile = pl.ds(pl.multiple_of(jnp.clip(at, 0, seq_local - 1) // TILE * TILE, TILE), TILE)
            for i in range(2):
                new = new_f32[i, pl.ds(reqs.start + r, 1), :]
                old = kv[h, r, i, tile].astype(jnp.float32)
                kv[h, r, i, tile] = jnp.where(row == at - tile.start, new, old).astype(kv.dtype)
            return carry

        lax.fori_loop(0, reqs.size, insert, 0)
        pltpu.make_async_copy(kv.at[h], blocks[h], out_sem.at[h]).start()
    for h in range(len(hops)):
        whole(kv.at[h], out_sem.at[h]).wait()


def unpack_kernel(n, reqs, *refs):
    blocks = refs[:n]
    k_out, v_out, raw, held, in_sem, out_sem = refs[-6:]
    me = lax.axis_index("tp")
    copies = []
    for j in (*HOPS, 0):
        head = lax.rem(me + n - j, n)
        copies.append(pltpu.make_async_copy(blocks[j], raw.at[:, :, head], in_sem.at[j]))
        copies[-1].start()
    for cp in copies:
        cp.wait()

    def finish(r, carry):
        for i, out in enumerate((k_out, v_out)):
            x = jnp.swapaxes(raw[r, i].astype(jnp.float32), 0, 1)
            held[i, r] = x.astype(held.dtype)
            pltpu.make_async_copy(held.at[i, r], out.at[reqs.start + r], out_sem.at[i]).start()
        return carry

    lax.fori_loop(0, reqs.size, finish, 0)
    for i in range(2):
        whole(held.at[i], out_sem.at[i]).wait()


def attend_kernel(lens_hbm, q_hbm, kn_hbm, vn_hbm, k_hbm, v_hbm, after_hbm, out_ref,
                  lens_ref, q_ref, new_in, new_f32, kv, in_sem, kv_sem):
    batch, seq_len, head_dim = k_hbm.shape
    small = (pltpu.make_async_copy(lens_hbm, lens_ref, in_sem.at[0]),
             pltpu.make_async_copy(q_hbm, q_ref, in_sem.at[1]),
             pltpu.make_async_copy(kn_hbm, new_in.at[0], in_sem.at[2]),
             pltpu.make_async_copy(vn_hbm, new_in.at[1], in_sem.at[3]))
    for cp in small:
        cp.start()

    def load(b, slot):
        pltpu.make_async_copy(k_hbm.at[b], kv.at[slot, 0], kv_sem.at[slot]).start()
        pltpu.make_async_copy(v_hbm.at[b], kv.at[slot, 1], kv_sem.at[slot]).start()

    load(0, 0)
    for cp in small:
        cp.wait()
    new_f32[...] = new_in[...].astype(jnp.float32)
    scale = head_dim ** -0.5
    pos = lax.broadcasted_iota(jnp.int32, (1, seq_len), 1)

    def attend(b, carry):
        slot = lax.rem(b, 2)

        @pl.when(b + 1 < batch)
        def _():
            load(b + 1, 1 - slot)

        whole(kv.at[slot], kv_sem.at[slot]).wait()
        length = lens_ref[b]
        q = q_ref[b]
        s = lax.dot_general(q, kv[slot, 0], (((1,), (1,)), ((), ())), preferred_element_type=jnp.float32) * scale
        s_new = jnp.sum(q.astype(jnp.float32) * new_f32[0, pl.ds(b, 1), :], axis=1, keepdims=True) * scale
        s = jnp.where(pos < length, s, MASK_VALUE)
        m = jnp.maximum(jnp.max(s, axis=1, keepdims=True), s_new)
        e = jnp.where(pos < length, jnp.exp(s - m), 0.0)
        e_new = jnp.exp(s_new - m)
        denom = jnp.sum(e, axis=1, keepdims=True) + e_new
        p = (e / denom).astype(kv.dtype)
        p_new = (e_new / denom).astype(kv.dtype).astype(jnp.float32)
        o = lax.dot_general(p, kv[slot, 1], (((1,), (0,)), ((), ())), preferred_element_type=jnp.float32)
        out_ref[b] = (o + p_new * new_f32[1, pl.ds(b, 1), :]).astype(out_ref.dtype)
        return carry

    lax.fori_loop(0, batch, attend, 0)


def spans(total, sizes):
    out, start = [], 0
    while start < total:
        size = min(sizes[min(len(out), len(sizes) - 1)], total - start)
        out.append(pl.ds(start, size))
        start += size
    return out


def packs(p):
    return (HOPS[:EARLY], (*HOPS[EARLY:], 0)) if p == 0 else ((*HOPS, 0),)


def cost(flops, moved):
    return pl.CostEstimate(flops=flops, bytes_accessed=moved, transcendentals=0)


def solution(mesh):
    n = mesh.shape["tp"]

    def layer(query, k_cache, v_cache, k_new, v_new, lens):
        batch, seq_len, kv_heads, head_dim = k_cache.shape
        seq_local = seq_len // n
        dtype = k_cache.dtype
        hbm = pl.BlockSpec(memory_space=pltpu.HBM)
        keys, values = (x.reshape(batch, seq_len, head_dim) for x in (k_cache, v_cache))
        new_k, new_v = (x.reshape(batch, head_dim) for x in (k_new, v_new))
        row_bytes = 2 * 2 * seq_len * head_dim

        def pack(reqs, hops, after):
            block = jax.ShapeDtypeStruct((reqs.size, 2, seq_local, head_dim), dtype)
            return pl.pallas_call(
                functools.partial(pack_kernel, n, reqs, hops, len(after)),
                out_shape=(block,) * len(hops),
                in_specs=[hbm] * (5 + len(after)),
                out_specs=(hbm,) * len(hops),
                scratch_shapes=[
                    pltpu.SMEM((batch,), jnp.int32),
                    pltpu.VMEM((2, batch, head_dim), dtype),
                    pltpu.VMEM((2, batch, head_dim), jnp.float32),
                    pltpu.VMEM((len(hops), *block.shape), dtype),
                    pltpu.SemaphoreType.DMA((2,)),
                    pltpu.SemaphoreType.DMA((len(hops),)),
                    pltpu.SemaphoreType.DMA((len(hops),)),
                ],
                compiler_params=pltpu.CompilerParams(vmem_limit_bytes=LESS_BYTES if after else VMEM_BYTES),
                cost_estimate=cost(0, 2 * reqs.size * row_bytes * len(hops) // n),
            )(lens, new_k, new_v, keys, values, *after)

        def unpack(reqs, blocks, outs):
            cache = jax.ShapeDtypeStruct((batch, seq_local, n * kv_heads, head_dim), dtype)
            return pl.pallas_call(
                functools.partial(unpack_kernel, n, reqs),
                out_shape=(cache, cache),
                in_specs=[hbm] * (n + len(outs)),
                out_specs=(hbm, hbm),
                scratch_shapes=[
                    pltpu.VMEM((reqs.size, 2, n, seq_local, head_dim), dtype),
                    pltpu.VMEM((2, reqs.size, seq_local, n * kv_heads, head_dim), dtype),
                    pltpu.SemaphoreType.DMA((n,)),
                    pltpu.SemaphoreType.DMA((2,)),
                ],
                input_output_aliases={n + i: i for i in range(len(outs))},
                compiler_params=pltpu.CompilerParams(vmem_limit_bytes=LESS_BYTES),
                cost_estimate=cost(0, 2 * reqs.size * row_bytes),
            )(*blocks, *outs)

        pieces = spans(batch, PIECES)
        arrived = []
        after = ()
        for p, reqs in enumerate(pieces):
            blocks = {}
            for hops in packs(p):
                packed = pack(reqs, hops, after)
                blocks.update(zip(hops, packed))
                after = (packed[-1],)
            for j in HOPS:
                blocks[j] = lax.ppermute(blocks[j], "tp", [(i, (i + j) % n) for i in range(n)])
            blocks = [blocks[j] for j in range(n)]
            arrived.append(blocks)

        group = query.shape[1]
        out = pl.pallas_call(
            attend_kernel,
            out_shape=jax.ShapeDtypeStruct(query.shape, query.dtype),
            in_specs=[hbm] * 7,
            out_specs=pl.BlockSpec(memory_space=pltpu.VMEM),
            scratch_shapes=[
                pltpu.SMEM((batch,), jnp.int32),
                pltpu.VMEM(query.shape, query.dtype),
                pltpu.VMEM((2, batch, head_dim), dtype),
                pltpu.VMEM((2, batch, head_dim), jnp.float32),
                pltpu.VMEM((2, 2, seq_len, head_dim), dtype),
                pltpu.SemaphoreType.DMA((4,)),
                pltpu.SemaphoreType.DMA((2,)),
            ],
            compiler_params=pltpu.CompilerParams(vmem_limit_bytes=LESS_BYTES),
            cost_estimate=cost(4 * batch * group * seq_len * head_dim, batch * row_bytes),
            name="attend",
        )(lens, query, new_k, new_v, keys, values, *after)

        outs = ()
        for reqs, blocks in zip(pieces, arrived):
            outs = unpack(reqs, blocks, outs)
        return out, *outs

    head_spec = P("dp", "tp")
    entry_spec = P("dp", None, "tp")
    return jax.shard_map(layer, mesh=mesh, in_specs=(head_spec, entry_spec, entry_spec, head_spec, head_spec, P("dp")), out_specs=(head_spec, P("dp", "tp"), P("dp", "tp")), check_vma=False)
```

time: 363 us -> 277 us (0.76)
  blocking collectives: 225 us -> 0 us
  waiting for transfers between devices: 11.6 us -> 153 us
  Pallas kernels: 0 us -> 70.9 us
  local copies, waits for them, and re-layouts: 50.4 us -> 2.8 us
  starting transfers between devices: 6.09 us -> 48.8 us
  other arithmetic: 42.7 us -> 0 us
  between operations: 14.1 us -> 1.02 us
  matrix products: 11.6 us -> 0 us
    ppermute x0 -> x42, waiting for transfers between devices: none -> 153 us  [layer(): lax.ppermute(blocks[j], 'tp', [(i, (i + j) % n) for i in range(n)])]
    all_gather x1 -> x0, blocking collectives: 102 us -> none  [local_step(): q_all = lax.all_gather(query, 'tp', axis=1, tiled=True)]
    all_to_all x1 -> x0, blocking collectives: 99.4 us -> none  [local_step(): k_seq = lax.all_to_all(k_upd, 'tp', 1, 2, tiled=True)]
    pallas_call x0 -> x14, Pallas kernels: none -> 70.9 us  [the longest x1 26.6 us: layer(): pl.pallas_call(attend_kernel, out_shape=jax.ShapeDtypeStruct(query.shape,...]
    ppermute x0 -> x42, starting transfers between devices: none -> 48.8 us  [layer(): lax.ppermute(blocks[j], 'tp', [(i, (i + j) % n) for i in range(n)])]
    select_n x1 -> x0, other arithmetic: 35.1 us -> none  [local_step(): v_upd = jnp.where(new_slot, v_new[:, None], v_cache)]
    pmax x1 -> x0, blocking collectives: 22.8 us -> none  [local_step(): glob_max = lax.pmax(part_max, 'tp')]
    unnamed x7 -> x58, local copies, waits for them, and re-layouts: 25.2 us -> 2.8 us
  transfers between devices with their start and end apart: 2 -> 42, of which waited for: 1 -> 21; matrix products, arithmetic and copies ran while one was open for 12% -> 0% of each run, Pallas kernels for 0% -> 18%
where the time goes in v3:
time: 277 us; the launch traced here: 276 us
  waiting for transfers between devices  153 us (55%)
  Pallas kernels  70.9 us (26%)
  starting transfers between devices  48.8 us (18%)
  local copies, waits for them, and re-layouts  2.8 us (1%)
    ppermute x42, waiting for transfers between devices, layer(): lax.ppermute(blocks[j], 'tp', [(i, (i + j) % n) for i in range(n)])  153 us
    ppermute x42, starting transfers between devices, layer(): lax.ppermute(blocks[j], 'tp', [(i, (i + j) % n) for i in range(n)])  48.8 us
    pallas_call x1, Pallas kernels, layer(): pl.pallas_call(attend_kernel, out_shape=jax.ShapeDtypeStruct(query.shape,...  26.6 us
    pallas_call x6, Pallas kernels, unpack(): pl.pallas_call(functools.partial(unpack_kernel, n, reqs), out_shape=(cach...  22.5 us
    pallas_call x7, Pallas kernels, pack(): pl.pallas_call(functools.partial(pack_kernel, n, reqs, hops, len(after)),...  21.9 us
  transfers between devices with their start and end apart: 42, of which 21 were waited for; matrix products, arithmetic and copies ran while one was open for 0% of the time, Pallas kernels for 18%

profile of v3, /device:TPU:81, one launch (start us, length us, event | category | flops | bytes accessed | tf_op | source)
XLA Modules:
  0.0 276.1 jit_solution(3565122945598135531)
XLA Ops:
  8.2 4.9 %shard_map.88 = (bf16[10,2,128,128]{3,2,1,0:T(8,128)(2,1)}, bf16[10,2,128,128]{3,2,1,0:T(8,128)(2,1)}, bf16[10,2,128,128]{3,2,1,0:T(8,128)(2,1)}, bf16[10,2,128,...) custom-call(s32[32]{0:T(128)} %lens_hbm.15, ...), custom_call_target="tpu_custom_call" | custom-call | bytes 10485760 | tf_op jit(solution)/shard_map/pallas_call | solution.py:162
  13.1 4.8 %shard_map.89 = (bf16[10,2,128,128]{3,2,1,0:T(8,128)(2,1)}, bf16[10,2,128,128]{3,2,1,0:T(8,128)(2,1)}, bf16[10,2,128,128]{3,2,1,0:T(8,128)(2,1)}, bf16[10,2,128,...) custom-call(s32[32]{0:T(128)} %lens_hbm.15, ...), custom_call_target="tpu_custom_call" | custom-call | bytes 10485760 | tf_op jit(solution)/shard_map/pallas_call | solution.py:162
  20.6 3.9 %collective-permute-start.10 = (bf16[3,2,128,128]{3,2,1,0:T(8,128)(2,1)}, bf16[3,2,128,128]{3,2,1,0:T(8,128)(2,1)S(1)}, u32[]{:S(2)}, u32[]{:S(2)}) collective-permute-start(bf16[3,2,128,128]{3,2,1,0:T(8,128)(2,1)} %get-tuple-element.80), channel_id=1, source_target_pairs={{0,4},{1,5},{2,6},{3,7},{4,0},{5,1},{6,2},{7,3},{8,12},{9,13},{10,... | collective-permute-start | bytes 589832 | tf_op jit(solution)/shard_map/ppermute | solution.py:208
  32.3 3.8 %collective-permute-done.1.refs_2_ = bf16[1,2,128,128]{3,2,1,0:T(8,128)(2,1)S(1)} collective-permute-done((bf16[1,2,128,128]{3,2,1,0:T(8,128)(2,1)}, bf16[1,2,128,128]{3,2,1,0:T(8,128)(2,1)S(1)}, u32[]{:S(2)}, u32[]{:S(2)}) %collective-permute-start.1) | collective-permute-done | bytes 65568 | tf_op jit(solution)/shard_map/ppermute | solution.py:208
  40.0 5.3 %collective-permute-start.9 = (bf16[3,2,128,128]{3,2,1,0:T(8,128)(2,1)S(1)}, bf16[3,2,128,128]{3,2,1,0:T(8,128)(2,1)S(1)}, u32[]{:S(2)}, u32[]{:S(2)}) collective-permute-start(bf16[3,2,128,128]{3,2,1,0:T(8,128)(2,1)S(1)} %copy-done.28), channel_id=1, source_target_pairs={{0,3},{1,4},{2,5},{3,6},{4,7},{5,0},{6,1},{7,2},{8,11},{9,12},{10,... | collective-permute-start | bytes 589832 | tf_op jit(solution)/shard_map/ppermute | solution.py:208
  50.6 9.7 %collective-permute-done.8.refs_2_ = bf16[3,2,128,128]{3,2,1,0:T(8,128)(2,1)S(1)} collective-permute-done((bf16[3,2,128,128]{3,2,1,0:T(8,128)(2,1)}, bf16[3,2,128,128]{3,2,1,0:T(8,128)(2,1)S(1)}, u32[]{:S(2)}, u32[]{:S(2)}) %collective-permute-start.8) | collective-permute-done | bytes 196640 | tf_op jit(solution)/shard_map/ppermute | solution.py:208
  61.7 12.3 %collective-permute-done.36.refs_2_ = bf16[4,2,128,128]{3,2,1,0:T(8,128)(2,1)S(1)} collective-permute-done((bf16[4,2,128,128]{3,2,1,0:T(8,128)(2,1)}, bf16[4,2,128,128]{3,2,1,0:T(8,128)(2,1)S(1)}, u32[]{:S(2)}, u32[]{:S(2)}) %collective-permute-start.36) | collective-permute-done | bytes 262176 | tf_op jit(solution)/shard_map/ppermute | solution.py:208
  75.3 4.9 %collective-permute-start.30 = (bf16[4,2,128,128]{3,2,1,0:T(8,128)(2,1)}, bf16[4,2,128,128]{3,2,1,0:T(8,128)(2,1)S(1)}, u32[]{:S(2)}, u32[]{:S(2)}) collective-permute-start(bf16[4,2,128,128]{3,2,1,0:T(8,128)(2,1)} %get-tuple-element.100), channel_id=1, source_target_pairs={{0,3},{1,4},{2,5},{3,6},{4,7},{5,0},{6,1},{7,2},{8,11},{9,12},{10,... | collective-permute-start | bytes 786440 | tf_op jit(solution)/shard_map/ppermute | solution.py:208
  95.7 3.9 %collective-permute-start.23 = (bf16[10,2,128,128]{3,2,1,0:T(8,128)(2,1)}, bf16[10,2,128,128]{3,2,1,0:T(8,128)(2,1)}, u32[]{:S(2)}, u32[]{:S(2)}) collective-permute-start(bf16[10,2,128,128]{3,2,1,0:T(8,128)(2,1)} %get-tuple-element.93), channel_id=1, source_target_pairs={{0,3},{1,4},{2,5},{3,6},{4,7},{5,0},{6,1},{7,2},{8,11},{9,12},{10,... | collective-permute-start | bytes 1966088 | tf_op jit(solution)/shard_map/ppermute | solution.py:208
  99.7 6.0 %collective-permute-done.31.refs_4_ = bf16[4,2,128,128]{3,2,1,0:T(8,128)(2,1)S(1)} collective-permute-done((bf16[4,2,128,128]{3,2,1,0:T(8,128)(2,1)}, bf16[4,2,128,128]{3,2,1,0:T(8,128)(2,1)S(1)}, u32[]{:S(2)}, u32[]{:S(2)}) %collective-permute-start.31) | collective-permute-done | bytes 262176 | tf_op jit(solution)/shard_map/ppermute | solution.py:208
  105.8 15.7 %collective-permute-done.33.refs_6_ = bf16[4,2,128,128]{3,2,1,0:T(8,128)(2,1)S(1)} collective-permute-done((bf16[4,2,128,128]{3,2,1,0:T(8,128)(2,1)}, bf16[4,2,128,128]{3,2,1,0:T(8,128)(2,1)S(1)}, u32[]{:S(2)}, u32[]{:S(2)}) %collective-permute-start.33) | collective-permute-done | bytes 262176 | tf_op jit(solution)/shard_map/ppermute | solution.py:208
  122.9 6.0 %collective-permute-done.34.refs_7_ = bf16[4,2,128,128]{3,2,1,0:T(8,128)(2,1)S(1)} collective-permute-done((bf16[4,2,128,128]{3,2,1,0:T(8,128)(2,1)}, bf16[4,2,128,128]{3,2,1,0:T(8,128)(2,1)S(1)}, u32[]{:S(2)}, u32[]{:S(2)}) %collective-permute-start.34) | collective-permute-done | bytes 262176 | tf_op jit(solution)/shard_map/ppermute | solution.py:208
  133.5 10.0 %collective-permute-done.23.refs_3_ = bf16[10,2,128,128]{3,2,1,0:T(8,128)(2,1)} collective-permute-done((bf16[10,2,128,128]{3,2,1,0:T(8,128)(2,1)}, bf16[10,2,128,128]{3,2,1,0:T(8,128)(2,1)}, u32[]{:S(2)}, u32[]{:S(2)}) %collective-permute-start.23) | collective-permute-done | bytes 655392 | tf_op jit(solution)/shard_map/ppermute | solution.py:208
  143.5 18.5 %collective-permute-done.24.refs_4_ = bf16[10,2,128,128]{3,2,1,0:T(8,128)(2,1)} collective-permute-done((bf16[10,2,128,128]{3,2,1,0:T(8,128)(2,1)}, bf16[10,2,128,128]{3,2,1,0:T(8,128)(2,1)}, u32[]{:S(2)}, u32[]{:S(2)}) %collective-permute-start.24) | collective-permute-done | bytes 655392 | tf_op jit(solution)/shard_map/ppermute | solution.py:208
  163.1 8.9 %collective-permute-done.27.refs_7_ = bf16[10,2,128,128]{3,2,1,0:T(8,128)(2,1)} collective-permute-done((bf16[10,2,128,128]{3,2,1,0:T(8,128)(2,1)}, bf16[10,2,128,128]{3,2,1,0:T(8,128)(2,1)}, u32[]{:S(2)}, u32[]{:S(2)}) %collective-permute-start.27) | collective-permute-done | bytes 655392 | tf_op jit(solution)/shard_map/ppermute | solution.py:208
  173.3 16.8 %collective-permute-done.15.refs_2_ = bf16[10,2,128,128]{3,2,1,0:T(8,128)(2,1)} collective-permute-done((bf16[10,2,128,128]{3,2,1,0:T(8,128)(2,1)}, bf16[10,2,128,128]{3,2,1,0:T(8,128)(2,1)}, u32[]{:S(2)}, u32[]{:S(2)}) %collective-permute-start.15) | collective-permute-done | bytes 655392 | tf_op jit(solution)/shard_map/ppermute | solution.py:208
  190.1 9.6 %collective-permute-done.16.refs_3_ = bf16[10,2,128,128]{3,2,1,0:T(8,128)(2,1)} collective-permute-done((bf16[10,2,128,128]{3,2,1,0:T(8,128)(2,1)}, bf16[10,2,128,128]{3,2,1,0:T(8,128)(2,1)}, u32[]{:S(2)}, u32[]{:S(2)}) %collective-permute-start.16) | collective-permute-done | bytes 655392 | tf_op jit(solution)/shard_map/ppermute | solution.py:208
  199.7 4.0 %collective-permute-start.2 = (bf16[1,2,128,128]{3,2,1,0:T(8,128)(2,1)}, bf16[1,2,128,128]{3,2,1,0:T(8,128)(2,1)}, u32[]{:S(2)}, u32[]{:S(2)}) collective-permute-start(bf16[1,2,128,128]{3,2,1,0:T(8,128)(2,1)} %get-tuple-element.72), channel_id=1, source_target_pairs={{0,3},{1,4},{2,5},{3,6},{4,7},{5,0},{6,1},{7,2},{8,11},{9,12},{10,... | collective-permute-start | bytes 196616 | tf_op jit(solution)/shard_map/ppermute | solution.py:208
  203.7 13.7 %collective-permute-done.17.refs_4_ = bf16[10,2,128,128]{3,2,1,0:T(8,128)(2,1)} collective-permute-done((bf16[10,2,128,128]{3,2,1,0:T(8,128)(2,1)}, bf16[10,2,128,128]{3,2,1,0:T(8,128)(2,1)}, u32[]{:S(2)}, u32[]{:S(2)}) %collective-permute-start.17) | collective-permute-done | bytes 655392 | tf_op jit(solution)/shard_map/ppermute | solution.py:208
  217.5 6.3 %collective-permute-done.19.refs_6_ = bf16[10,2,128,128]{3,2,1,0:T(8,128)(2,1)} collective-permute-done((bf16[10,2,128,128]{3,2,1,0:T(8,128)(2,1)}, bf16[10,2,128,128]{3,2,1,0:T(8,128)(2,1)}, u32[]{:S(2)}, u32[]{:S(2)}) %collective-permute-start.19) | collective-permute-done | bytes 655392 | tf_op jit(solution)/shard_map/ppermute | solution.py:208
  227.0 26.6 %attend.1 = bf16[32,8,128]{2,1,0:T(8,128)(2,1)} custom-call(s32[32]{0:T(128)} %lens_hbm.15, bf16[32,8,128]{2,1,0:T(8,128)(2,1)} %q_hbm.1, bf16[32,128]{1,0:T(8,128)(2,1)} %bitcast.27, bf16[32,128]{1,0:T(8,128)(2,1)} %bitcast.35, bf16[32,1024,128]{2,1,0:T(8,128)(2,1)} %bitcast.11, bf16[32,1024,128]{2,1,0:T(8,128)(2,1)} %bitcast.19, ...), custom_call_target="tpu_custom_call" | custom-call | flops 134217728 | bytes 16777216 | tf_op jit(solution)/shard_map/attend/pallas_call | solution.py:213
  256.8 3.2 %shard_map.93 = (bf16[32,128,8,128]{3,2,1,0:T(8,128)(2,1)}, bf16[32,128,8,128]{3,2,1,0:T(8,128)(2,1)}) custom-call(bf16[4,2,128,128]{3,2,1,0:T(8,128)(2,1)} %get-tuple-element.65.refs_0_, bf16[4,2,128,128]{3,2,1,0:T(8,128)(2,1)} %copy-done.2, bf16[4,2,128,128]{3,2,1,0:T(8,128)(2,1)} %copy-done.3, ...), custom_call_target="tpu_custom_call", output_to_operand_aliasing={{0}: (8, {}), {1}: (9, {})} | custom-call | bytes 4194304 | tf_op jit(solution)/shard_map/pallas_call | solution.py:182
  260.0 5.5 %shard_map.94 = (bf16[32,128,8,128]{3,2,1,0:T(8,128)(2,1)}, bf16[32,128,8,128]{3,2,1,0:T(8,128)(2,1)}) custom-call(bf16[10,2,128,128]{3,2,1,0:T(8,128)(2,1)} %get-tuple-element.66.refs_0_, bf16[10,2,128,128]{3,2,1,0:T(8,128)(2,1)} %copy-done, bf16[10,2,128,128]{3,2,1,0:T(8,128)(2,1)} %copy-done.1, ...), custom_call_target="tpu_custom_call", output_to_operand_aliasing={{0}: (8, {}), {1}: (9, {})} | custom-call | bytes 10485760 | tf_op jit(solution)/shard_map/pallas_call | solution.py:182
  265.5 5.5 %shard_map.95 = (bf16[32,128,8,128]{3,2,1,0:T(8,128)(2,1)}, bf16[32,128,8,128]{3,2,1,0:T(8,128)(2,1)}) custom-call(bf16[10,2,128,128]{3,2,1,0:T(8,128)(2,1)} %get-tuple-element.67.refs_0_, bf16[10,2,128,128]{3,2,1,0:T(8,128)(2,1)} %collective-permute-done.14.refs_1_, ...), custom_call_target="tpu_custom_call", output_to_operand_aliasing={{0}: (8, {}), {1}: (9, {})} | custom-call | bytes 10485760 | tf_op jit(solution)/shard_map/pallas_call | solution.py:182
  (132 shorter events, 65.4 us)
Async XLA Ops:
  36.1 25.5 %collective-permute-start.35 = (bf16[4,2,128,128]{3,2,1,0:T(8,128)(2,1)}, bf16[4,2,128,128]{3,2,1,0:T(8,128)(2,1)S(1)}, u32[]{:S(2)}, u32[]{:S(2)}) collective-permute-start(bf16[4,2,128,128]{3,2,1,0:T(8,128)(2,1)} %get-tuple-element.105), channel_id=1, source_target_pairs={{0,1},{1,2},{2,3},{3,4},{4,5},{5,6},{6,7},{7,0},{8,9},{9,10},{10,1... | collective-permute-start | bytes 786440 | tf_op jit(solution)/shard_map/ppermute | solution.py:208
  45.4 28.6 %collective-permute-start.36 = (bf16[4,2,128,128]{3,2,1,0:T(8,128)(2,1)}, bf16[4,2,128,128]{3,2,1,0:T(8,128)(2,1)S(1)}, u32[]{:S(2)}, u32[]{:S(2)}) collective-permute-start(bf16[4,2,128,128]{3,2,1,0:T(8,128)(2,1)} %get-tuple-element.106), channel_id=1, source_target_pairs={{0,2},{1,3},{2,4},{3,5},{4,6},{5,7},{6,0},{7,1},{8,10},{9,11},{10,... | collective-permute-start | bytes 786440 | tf_op jit(solution)/shard_map/ppermute | solution.py:208
  48.6 26.5 %collective-permute-start.37 = (bf16[4,2,128,128]{3,2,1,0:T(8,128)(2,1)S(1)}, bf16[4,2,128,128]{3,2,1,0:T(8,128)(2,1)S(1)}, u32[]{:S(2)}, u32[]{:S(2)}) collective-permute-start(bf16[4,2,128,128]{3,2,1,0:T(8,128)(2,1)S(1)} %copy-done.27), channel_id=1, source_target_pairs={{0,3},{1,4},{2,5},{3,6},{4,7},{5,0},{6,1},{7,2},{8,11},{9,12},{10,... | collective-permute-start | bytes 786440 | tf_op jit(solution)/shard_map/ppermute | solution.py:208
  80.2 25.4 %collective-permute-start.31 = (bf16[4,2,128,128]{3,2,1,0:T(8,128)(2,1)}, bf16[4,2,128,128]{3,2,1,0:T(8,128)(2,1)S(1)}, u32[]{:S(2)}, u32[]{:S(2)}) collective-permute-start(bf16[4,2,128,128]{3,2,1,0:T(8,128)(2,1)} %get-tuple-element.101), channel_id=1, source_target_pairs={{0,4},{1,5},{2,6},{3,7},{4,0},{5,1},{6,2},{7,3},{8,12},{9,13},{10,... | collective-permute-start | bytes 786440 | tf_op jit(solution)/shard_map/ppermute | solution.py:208
  83.1 22.5 %collective-permute-start.32 = (bf16[4,2,128,128]{3,2,1,0:T(8,128)(2,1)}, bf16[4,2,128,128]{3,2,1,0:T(8,128)(2,1)S(1)}, u32[]{:S(2)}, u32[]{:S(2)}) collective-permute-start(bf16[4,2,128,128]{3,2,1,0:T(8,128)(2,1)} %get-tuple-element.102), channel_id=1, source_target_pairs={{0,5},{1,6},{2,7},{3,0},{4,1},{5,2},{6,3},{7,4},{8,13},{9,14},{10,... | collective-permute-start | bytes 786440 | tf_op jit(solution)/shard_map/ppermute | solution.py:208
  84.5 44.9 %collective-permute-start.21 = (bf16[10,2,128,128]{3,2,1,0:T(8,128)(2,1)}, bf16[10,2,128,128]{3,2,1,0:T(8,128)(2,1)S(1)}, u32[]{:S(2)}, u32[]{:S(2)}) collective-permute-start(bf16[10,2,128,128]{3,2,1,0:T(8,128)(2,1)} %get-tuple-element.91), channel_id=1, source_target_pairs={{0,1},{1,2},{2,3},{3,4},{4,5},{5,6},{6,7},{7,0},{8,9},{9,10},{10,1... | collective-permute-start | bytes 1966088 | tf_op jit(solution)/shard_map/ppermute | solution.py:208
  90.7 41.4 %collective-permute-start.22 = (bf16[10,2,128,128]{3,2,1,0:T(8,128)(2,1)}, bf16[10,2,128,128]{3,2,1,0:T(8,128)(2,1)S(1)}, u32[]{:S(2)}, u32[]{:S(2)}) collective-permute-start(bf16[10,2,128,128]{3,2,1,0:T(8,128)(2,1)} %get-tuple-element.92), channel_id=1, source_target_pairs={{0,2},{1,3},{2,4},{3,5},{4,6},{5,7},{6,0},{7,1},{8,10},{9,11},{10,... | collective-permute-start | bytes 1966088 | tf_op jit(solution)/shard_map/ppermute | solution.py:208
  95.7 47.7 %collective-permute-start.23 = (bf16[10,2,128,128]{3,2,1,0:T(8,128)(2,1)}, bf16[10,2,128,128]{3,2,1,0:T(8,128)(2,1)}, u32[]{:S(2)}, u32[]{:S(2)}) collective-permute-start(bf16[10,2,128,128]{3,2,1,0:T(8,128)(2,1)} %get-tuple-element.93), channel_id=1, source_target_pairs={{0,3},{1,4},{2,5},{3,6},{4,7},{5,0},{6,1},{7,2},{8,11},{9,12},{10,... | collective-permute-start | bytes 1966088 | tf_op jit(solution)/shard_map/ppermute | solution.py:208
  105.6 56.3 %collective-permute-start.24 = (bf16[10,2,128,128]{3,2,1,0:T(8,128)(2,1)}, bf16[10,2,128,128]{3,2,1,0:T(8,128)(2,1)}, u32[]{:S(2)}, u32[]{:S(2)}) collective-permute-start(bf16[10,2,128,128]{3,2,1,0:T(8,128)(2,1)} %get-tuple-element.94), channel_id=1, source_target_pairs={{0,4},{1,5},{2,6},{3,7},{4,0},{5,1},{6,2},{7,3},{8,12},{9,13},{10,... | collective-permute-start | bytes 1966088 | tf_op jit(solution)/shard_map/ppermute | solution.py:208
  128.9 33.0 %collective-permute-start.25 = (bf16[10,2,128,128]{3,2,1,0:T(8,128)(2,1)}, bf16[10,2,128,128]{3,2,1,0:T(8,128)(2,1)}, u32[]{:S(2)}, u32[]{:S(2)}) collective-permute-start(bf16[10,2,128,128]{3,2,1,0:T(8,128)(2,1)} %get-tuple-element.95), channel_id=1, source_target_pairs={{0,5},{1,6},{2,7},{3,0},{4,1},{5,2},{6,3},{7,4},{8,13},{9,14},{10,... | collective-permute-start | bytes 1966088 | tf_op jit(solution)/shard_map/ppermute | solution.py:208
  129.3 32.8 %collective-permute-start.26 = (bf16[10,2,128,128]{3,2,1,0:T(8,128)(2,1)}, bf16[10,2,128,128]{3,2,1,0:T(8,128)(2,1)}, u32[]{:S(2)}, u32[]{:S(2)}) collective-permute-start(bf16[10,2,128,128]{3,2,1,0:T(8,128)(2,1)} %get-tuple-element.96), channel_id=1, source_target_pairs={{0,6},{1,7},{2,0},{3,1},{4,2},{5,3},{6,4},{7,5},{8,14},{9,15},{10,... | collective-permute-start | bytes 1966088 | tf_op jit(solution)/shard_map/ppermute | solution.py:208
  132.1 39.9 %collective-permute-start.27 = (bf16[10,2,128,128]{3,2,1,0:T(8,128)(2,1)}, bf16[10,2,128,128]{3,2,1,0:T(8,128)(2,1)}, u32[]{:S(2)}, u32[]{:S(2)}) collective-permute-start(bf16[10,2,128,128]{3,2,1,0:T(8,128)(2,1)} %get-tuple-element.97), channel_id=1, source_target_pairs={{0,7},{1,0},{2,1},{3,2},{4,3},{5,4},{6,5},{7,6},{8,15},{9,8},{10,9... | collective-permute-start | bytes 1966088 | tf_op jit(solution)/shard_map/ppermute | solution.py:208
  143.5 28.5 %collective-permute-start.14 = (bf16[10,2,128,128]{3,2,1,0:T(8,128)(2,1)}, bf16[10,2,128,128]{3,2,1,0:T(8,128)(2,1)}, u32[]{:S(2)}, u32[]{:S(2)}) collective-permute-start(bf16[10,2,128,128]{3,2,1,0:T(8,128)(2,1)} %get-tuple-element.84), channel_id=1, source_target_pairs={{0,1},{1,2},{2,3},{3,4},{4,5},{5,6},{6,7},{7,0},{8,9},{9,10},{10,1... | collective-permute-start | bytes 1966088 | tf_op jit(solution)/shard_map/ppermute | solution.py:208
  162.0 28.2 %collective-permute-start.15 = (bf16[10,2,128,128]{3,2,1,0:T(8,128)(2,1)}, bf16[10,2,128,128]{3,2,1,0:T(8,128)(2,1)}, u32[]{:S(2)}, u32[]{:S(2)}) collective-permute-start(bf16[10,2,128,128]{3,2,1,0:T(8,128)(2,1)} %get-tuple-element.85), channel_id=1, source_target_pairs={{0,2},{1,3},{2,4},{3,5},{4,6},{5,7},{6,0},{7,1},{8,10},{9,11},{10,... | collective-permute-start | bytes 1966088 | tf_op jit(solution)/shard_map/ppermute | solution.py:208
  162.0 37.7 %collective-permute-start.16 = (bf16[10,2,128,128]{3,2,1,0:T(8,128)(2,1)}, bf16[10,2,128,128]{3,2,1,0:T(8,128)(2,1)}, u32[]{:S(2)}, u32[]{:S(2)}) collective-permute-start(bf16[10,2,128,128]{3,2,1,0:T(8,128)(2,1)} %get-tuple-element.86), channel_id=1, source_target_pairs={{0,3},{1,4},{2,5},{3,6},{4,7},{5,0},{6,1},{7,2},{8,11},{9,12},{10,... | collective-permute-start | bytes 1966088 | tf_op jit(solution)/shard_map/ppermute | solution.py:208
  162.1 55.3 %collective-permute-start.17 = (bf16[10,2,128,128]{3,2,1,0:T(8,128)(2,1)}, bf16[10,2,128,128]{3,2,1,0:T(8,128)(2,1)}, u32[]{:S(2)}, u32[]{:S(2)}) collective-permute-start(bf16[10,2,128,128]{3,2,1,0:T(8,128)(2,1)} %get-tuple-element.87), channel_id=1, source_target_pairs={{0,4},{1,5},{2,6},{3,7},{4,0},{5,1},{6,2},{7,3},{8,12},{9,13},{10,... | collective-permute-start | bytes 1966088 | tf_op jit(solution)/shard_map/ppermute | solution.py:208
  172.0 45.5 %collective-permute-start.18 = (bf16[10,2,128,128]{3,2,1,0:T(8,128)(2,1)}, bf16[10,2,128,128]{3,2,1,0:T(8,128)(2,1)}, u32[]{:S(2)}, u32[]{:S(2)}) collective-permute-start(bf16[10,2,128,128]{3,2,1,0:T(8,128)(2,1)} %get-tuple-element.88), channel_id=1, source_target_pairs={{0,5},{1,6},{2,7},{3,0},{4,1},{5,2},{6,3},{7,4},{8,13},{9,14},{10,... | collective-permute-start | bytes 1966088 | tf_op jit(solution)/shard_map/ppermute | solution.py:208
  172.0 51.8 %collective-permute-start.19 = (bf16[10,2,128,128]{3,2,1,0:T(8,128)(2,1)}, bf16[10,2,128,128]{3,2,1,0:T(8,128)(2,1)}, u32[]{:S(2)}, u32[]{:S(2)}) collective-permute-start(bf16[10,2,128,128]{3,2,1,0:T(8,128)(2,1)} %get-tuple-element.89), channel_id=1, source_target_pairs={{0,6},{1,7},{2,0},{3,1},{4,2},{5,3},{6,4},{7,5},{8,14},{9,15},{10,... | collective-permute-start | bytes 1966088 | tf_op jit(solution)/shard_map/ppermute | solution.py:208
  190.1 36.9 %collective-permute-start.20 = (bf16[10,2,128,128]{3,2,1,0:T(8,128)(2,1)}, bf16[10,2,128,128]{3,2,1,0:T(8,128)(2,1)}, u32[]{:S(2)}, u32[]{:S(2)}) collective-permute-start(bf16[10,2,128,128]{3,2,1,0:T(8,128)(2,1)} %get-tuple-element.90), channel_id=1, source_target_pairs={{0,7},{1,0},{2,1},{3,2},{4,3},{5,4},{6,5},{7,6},{8,15},{9,8},{10,9... | collective-permute-start | bytes 1966088 | tf_op jit(solution)/shard_map/ppermute | solution.py:208
  199.7 74.3 %collective-permute-start.2 = (bf16[1,2,128,128]{3,2,1,0:T(8,128)(2,1)}, bf16[1,2,128,128]{3,2,1,0:T(8,128)(2,1)}, u32[]{:S(2)}, u32[]{:S(2)}) collective-permute-start(bf16[1,2,128,128]{3,2,1,0:T(8,128)(2,1)} %get-tuple-element.72), channel_id=1, source_target_pairs={{0,3},{1,4},{2,5},{3,6},{4,7},{5,0},{6,1},{7,2},{8,11},{9,12},{10,... | collective-permute-start | bytes 196616 | tf_op jit(solution)/shard_map/ppermute | solution.py:208
  217.4 56.6 %collective-permute-start.3 = (bf16[1,2,128,128]{3,2,1,0:T(8,128)(2,1)}, bf16[1,2,128,128]{3,2,1,0:T(8,128)(2,1)}, u32[]{:S(2)}, u32[]{:S(2)}) collective-permute-start(bf16[1,2,128,128]{3,2,1,0:T(8,128)(2,1)} %get-tuple-element.73), channel_id=1, source_target_pairs={{0,4},{1,5},{2,6},{3,7},{4,0},{5,1},{6,2},{7,3},{8,12},{9,13},{10,... | collective-permute-start | bytes 196616 | tf_op jit(solution)/shard_map/ppermute | solution.py:208
  217.5 56.5 %collective-permute-start.4 = (bf16[1,2,128,128]{3,2,1,0:T(8,128)(2,1)}, bf16[1,2,128,128]{3,2,1,0:T(8,128)(2,1)}, u32[]{:S(2)}, u32[]{:S(2)}) collective-permute-start(bf16[1,2,128,128]{3,2,1,0:T(8,128)(2,1)} %get-tuple-element.74), channel_id=1, source_target_pairs={{0,5},{1,6},{2,7},{3,0},{4,1},{5,2},{6,3},{7,4},{8,13},{9,14},{10,... | collective-permute-start | bytes 196616 | tf_op jit(solution)/shard_map/ppermute | solution.py:208
  223.8 50.2 %collective-permute-start.5 = (bf16[1,2,128,128]{3,2,1,0:T(8,128)(2,1)}, bf16[1,2,128,128]{3,2,1,0:T(8,128)(2,1)}, u32[]{:S(2)}, u32[]{:S(2)}) collective-permute-start(bf16[1,2,128,128]{3,2,1,0:T(8,128)(2,1)} %get-tuple-element.75), channel_id=1, source_target_pairs={{0,6},{1,7},{2,0},{3,1},{4,2},{5,3},{6,4},{7,5},{8,14},{9,15},{10,... | collective-permute-start | bytes 196616 | tf_op jit(solution)/shard_map/ppermute | solution.py:208
  227.0 47.1 %collective-permute-start.6 = (bf16[1,2,128,128]{3,2,1,0:T(8,128)(2,1)}, bf16[1,2,128,128]{3,2,1,0:T(8,128)(2,1)}, u32[]{:S(2)}, u32[]{:S(2)}) collective-permute-start(bf16[1,2,128,128]{3,2,1,0:T(8,128)(2,1)} %get-tuple-element.76), channel_id=1, source_target_pairs={{0,7},{1,0},{2,1},{3,2},{4,3},{5,4},{6,5},{7,6},{8,15},{9,8},{10,9... | collective-permute-start | bytes 196616 | tf_op jit(solution)/shard_map/ppermute | solution.py:208
  (47 other events, 1405.4 us)
